TPU v7x, 32 devices: a whole 2x2x4 slice. The times are simulated.
32 devices in a mesh: shard: 16 (over z, x, core), task: 2 (over y).
Axes of the slice: x: 2, y: 2, z: 4, core: 2. Of those that a mesh axis runs over, the one named last changes fastest.
Arguments:
- task_deltas: bfloat16 [2, 4, 256, 16384], P('task', None, 'shard')
- rank_scores: int32 [2, 4, 256, 16384], P('task', None, 'shard'), may hold values from 0 to 1073741823
- keep_limits: int32 [2, 4, 8], P('task'), may hold values from 268435456 to 805306367
Outputs:
- merged: bfloat16 [4, 256, 16384], P(None, 'shard', 'task')
All inputs are finite; a program needn't handle non-finite values.
Results may differ from a plain program's by a relative error of at most 0.0051.
Values may be sent and summed in bfloat16 or wider, within the bound.
No kernel may reach another device: no remote copies, remote signals or barrier semaphores. Data moves between devices by JAX's collectives and lax.ppermute only.
A program may use at most 64 MiB of HBM per device.

v0:
```python
import jax
import jax.numpy as jnp
from jax import lax
from jax.sharding import PartitionSpec as P

EXPERTS = 8
FF = 16384


def swapped(value, axis, stride):
    mask = 2**stride
    pairs = [(source, source ^ mask) for source in range(lax.axis_size(axis))]
    return lax.ppermute(value, axis, pairs)


def keep_probability(column_sums, grand_sum, row_total):
    column_mean = column_sums / row_total
    grand_mean = grand_sum / (EXPERTS * row_total * FF)
    return (0.2 + 0.7 * column_mean / (column_mean + grand_mean)).astype(jnp.bfloat16)


def on_device(task_deltas, rank_scores, keep_limits):
    groups = lax.axis_size("shard") // EXPERTS
    expert = lax.axis_index("shard") // groups
    row_count = task_deltas.shape[2]
    rows_whole = row_count * groups
    width_all = task_deltas.shape[3]
    selector = jnp.arange(EXPERTS, dtype=jnp.int32) == expert
    results = []
    for layer_at in range(task_deltas.shape[1]):
        change = task_deltas[0, layer_at].astype(jnp.float32)
        magnitude = jnp.sum(jnp.abs(change), axis=0)
        group_total = magnitude
        for bit_at in range(groups.bit_length() - 1):
            group_total = group_total + swapped(group_total, "shard", bit_at)
        grand_sum = lax.psum(jnp.sum(magnitude), "shard")
        rounded = lax.optimization_barrier(keep_probability(group_total, grand_sum, rows_whole))
        probability = rounded.astype(jnp.float32)
        own_limit = jnp.sum(jnp.where(selector, keep_limits[0, layer_at], 0))
        retained = jnp.where(
            rank_scores[0, layer_at] < own_limit, change / probability[None, :], jnp.float32(0.0)
        )
        summed = lax.psum(retained, "task")
        columns = width_all // lax.axis_size("task")
        portion = lax.dynamic_slice_in_dim(summed, lax.axis_index("task") * columns, columns, 1)
        results.append(portion.astype(jnp.bfloat16))
    return jnp.stack(results)


def solution(mesh):
    return jax.shard_map(
        on_device,
        mesh=mesh,
        in_specs=(
            P("task", None, "shard", None),
            P("task", None, "shard", None),
            P("task", None, None),
        ),
        out_specs=P(None, "shard", "task"),
        check_vma=False,
    )
```

profile of v0, /device:TPU:0, one launch (start us, length us, event | category | flops | bytes accessed | tf_op | source)
XLA Modules:
  0.0 146.4 jit_solution(15803664491565942427)
XLA Ops:
  0.0 0.0 copy-start
  0.0 0.0 copy-start.1
  0.0 3.3 %fusion = (f32[]{:T(128)}, f32[]{:T(128)}, f32[]{:T(128)}, f32[]{:T(128)}, f32[16384]{0:T(1024)S(1)}, /*index=5*/f32[16384]{0:T(1024)S(1)}, f32[16384]{0:T(1024)S(1)}, f32[16384]{0:T(1024)S(1)}) fusion(bf16[1,4,16,16384]{3,2,1,0:T(8,128)(2,1)} %param.3), kind=kLoop, calls=%fused_computation.8 | loop fusion | flops 4128764 | bytes 2359312 | tf_op jit(solution)/shard_map/reduce_sum | solution.py:36
  3.3 0.5 collective-permute-start.1
  3.8 0.0 collective-permute-start
  3.8 0.5 collective-permute-start.3
  4.3 0.0 collective-permute-start.2
  4.3 35.8 %all-reduce = (f32[]{:T(128)}, f32[]{:T(128)}, f32[]{:T(128)}, f32[]{:T(128)}) all-reduce(f32[]{:T(128)} %get-tuple-element.8, f32[]{:T(128)} %get-tuple-element.7, f32[]{:T(128)} %get-tuple-element.6, f32[]{:T(128)} %get-tuple-element.5), channel_id=1, replica_groups=mesh['shard'=16,'task'=2] {'shard'}, use_global_device_ids=true, to_apply=%region_18.19 | all-reduce | flops 4 | bytes 32 | tf_op jit(solution)/shard_map/psum | solution.py:36
  42.6 0.0 copy-done.1
  42.6 0.7 fusion.23
  43.3 0.0 collective-permute-done.1
  43.4 0.0 collective-permute-done
  43.4 0.0 collective-permute-done.3
  43.5 0.0 collective-permute-done.2
  43.5 0.0 copy-done
  43.6 6.6 %fusion.8 = (f32[16,16384]{1,0:T(8,128)S(1)}, f32[16,16384]{1,0:T(8,128)}, f32[16,16384]{1,0:T(8,128)}, f32[16,16384]{1,0:T(8,128)}) fusion(s32[1,4,16,16384]{3,2,1,0:T(8,128)} %param.4, f32[16384]{0:T(1024)S(1)} %convert_element_type.63, s32[]{:T(128)} %get-tuple-element.13, bf16[1,4,16,16384]{3,2,1,0:T(8,128)(2,1)S(1)} %copy-done, ...), kind=kLoop, calls=%fused_computation.16 | loop fusion | flops 4194304 | bytes 10747920 | tf_op jit(solution)/shard_map/jit(_where)/select_n | solution.py:40
  50.2 95.0 %all-reduce.3 = (bf16[16,16384]{1,0:T(8,128)(2,1)S(1)}, bf16[16,16384]{1,0:T(8,128)(2,1)S(1)}, bf16[16,16384]{1,0:T(8,128)(2,1)S(1)}, bf16[16,16384]{1,0:T(8,128)(2,1)S(1)}) all-reduce(f32[16,16384]{1,0:T(8,128)} %get-tuple-element.27, f32[16,16384]{1,0:T(8,128)} %get-tuple-element.28, ...), channel_id=1, replica_groups=mesh['shard'=16,'task'=2] {'task'}, use_global_device_ids=true, to_apply=%region_19.20 | all-reduce | flops 1048576 | bytes 6291456 | tf_op jit(solution)/shard_map/psum | solution.py:43
  145.3 1.1 pad_maximum_fusion
  (10 shorter events, 0.2 us)
Async XLA Ops:
  0.0 43.6 %copy-start = (bf16[1,4,16,16384]{3,2,1,0:T(8,128)(2,1)S(1)}, bf16[1,4,16,16384]{3,2,1,0:T(8,128)(2,1)}, u32[]{:S(2)}) copy-start(bf16[1,4,16,16384]{3,2,1,0:T(8,128)(2,1)} %param.3) | copy-start | bytes 6291460
  0.0 42.6 %copy-start.1 = (s32[1,4,8]{2,1,0:T(4,128)S(1)}, s32[1,4,8]{2,1,0:T(4,128)}, u32[]{:S(2)}) copy-start(s32[1,4,8]{2,1,0:T(4,128)} %param.5) | copy-start | bytes 388
  3.3 40.0 %collective-permute-start.1 = (f32[16384]{0:T(1024)S(1)}, f32[16384]{0:T(1024)S(1)}, u32[]{:S(2)}, u32[]{:S(2)}) collective-permute-start(f32[16384]{0:T(1024)S(1)} %get-tuple-element.9), channel_id=1, source_target_pairs={{0,2},{2,0},{4,6},{6,4},{8,10},{10,8},{12,14},{14,12},{16,18},{18,... | collective-permute-start | bytes 196616 | tf_op jit(solution)/shard_map/ppermute | solution.py:13
  3.8 39.5 %collective-permute-start = (f32[16384]{0:T(1024)S(1)}, f32[16384]{0:T(1024)S(1)}, u32[]{:S(2)}, u32[]{:S(2)}) collective-permute-start(f32[16384]{0:T(1024)S(1)} %get-tuple-element.10), channel_id=1, source_target_pairs={{0,2},{2,0},{4,6},{6,4},{8,10},{10,8},{12,14},{14,12},{16,18},{18,... | collective-permute-start | bytes 196616 | tf_op jit(solution)/shard_map/ppermute | solution.py:13
  3.8 39.6 %collective-permute-start.3 = (f32[16384]{0:T(1024)S(1)}, f32[16384]{0:T(1024)S(1)}, u32[]{:S(2)}, u32[]{:S(2)}) collective-permute-start(f32[16384]{0:T(1024)S(1)} %get-tuple-element.11), channel_id=1, source_target_pairs={{0,2},{2,0},{4,6},{6,4},{8,10},{10,8},{12,14},{14,12},{16,18},{18,... | collective-permute-start | bytes 196616 | tf_op jit(solution)/shard_map/ppermute | solution.py:13
  4.3 39.2 %collective-permute-start.2 = (f32[16384]{0:T(1024)S(1)}, f32[16384]{0:T(1024)S(1)}, u32[]{:S(2)}, u32[]{:S(2)}) collective-permute-start(f32[16384]{0:T(1024)S(1)} %get-tuple-element.12), channel_id=1, source_target_pairs={{0,2},{2,0},{4,6},{6,4},{8,10},{10,8},{12,14},{14,12},{16,18},{18,... | collective-permute-start | bytes 196616 | tf_op jit(solution)/shard_map/ppermute | solution.py:13
where the time goes:
time: 147 us; the launch traced here: 146 us
  blocking collectives  131 us (89%)
  other arithmetic  11.8 us (8%)
  between operations  2.65 us (2%)
    psum x1, blocking collectives, on_device(): summed = lax.psum(retained, 'task')  95 us
    psum x1, blocking collectives, on_device(): grand_sum = lax.psum(jnp.sum(magnitude), 'shard')  35.8 us
    select_n x1, other arithmetic, on_device(): jnp.where(rank_scores[0, layer_at] < own_limit, change / probability[None...  6.62 us
    reduce_sum x1, other arithmetic, on_device(): grand_sum = lax.psum(jnp.sum(magnitude), 'shard')  3.31 us
  transfers between devices with their start and end apart: 4, of which 0 were waited for; matrix products, arithmetic and copies ran while one was open for 1% of the time, Pallas kernels for 0%

commit v1 on v0

--- a/solution.py
+++ b/solution.py
@@ -40,7 +40,7 @@
         retained = jnp.where(
             rank_scores[0, layer_at] < own_limit, change / probability[None, :], jnp.float32(0.0)
         )
-        summed = lax.psum(retained, "task")
+        summed = jnp.sum(lax.all_gather(retained, "task"), axis=0)
         columns = width_all // lax.axis_size("task")
         portion = lax.dynamic_slice_in_dim(summed, lax.axis_index("task") * columns, columns, 1)
         results.append(portion.astype(jnp.bfloat16))

time: 147 us -> 201 us (1.37)
  waiting for transfers between devices: 0.01 us -> 129 us
  blocking collectives: 131 us -> 35.8 us
  between operations: 2.65 us -> 15.8 us
  other arithmetic: 11.8 us -> 19.4 us
    all_gather x0 -> x4, waiting for transfers between devices: none -> 127 us  [on_device(): summed = jnp.sum(lax.all_gather(retained, 'task'), axis=0)]
    psum x1 -> x0, blocking collectives: 95 us -> none  [on_device(): summed = lax.psum(retained, 'task')]
    reduce_sum x0 -> x4, other arithmetic: none -> 7 us  [on_device(): summed = jnp.sum(lax.all_gather(retained, 'task'), axis=0)]
  transfers between devices with their start and end apart: 4 -> 8, of which waited for: 0 -> 4; matrix products, arithmetic and copies ran while one was open for 1% -> 3% of each run, Pallas kernels for 0% -> 0%
where the time goes in v1:
time: 201 us
  waiting for transfers between devices  129 us (64%)
  blocking collectives  35.8 us (18%)
  other arithmetic  19.4 us (10%)
  between operations  15.8 us (8%)
    all_gather x4, waiting for transfers between devices, on_device(): summed = jnp.sum(lax.all_gather(retained, 'task'), axis=0)  127 us
    psum x1, blocking collectives, on_device(): grand_sum = lax.psum(jnp.sum(magnitude), 'shard')  35.8 us
    select_n x1, other arithmetic, on_device(): jnp.where(rank_scores[0, layer_at] < own_limit, change / probability[None...  7.13 us
    reduce_sum x4, other arithmetic, on_device(): summed = jnp.sum(lax.all_gather(retained, 'task'), axis=0)  7 us
  transfers between devices with their start and end apart: 8, of which 4 were waited for; matrix products, arithmetic and copies ran while one was open for 3% of the time, Pallas kernels for 0%

profile of v1, /device:TPU:0, one launch (start us, length us, event | category | flops | bytes accessed | tf_op | source)
XLA Modules:
  0.0 201.1 jit_solution(18045789110461857311)
XLA Ops:
  6.5 0.0 copy-start
  6.5 0.0 copy-start.1
  6.5 0.0 all-gather.5.cloned.1.call-start
  6.5 3.3 %fusion = (f32[]{:T(128)}, f32[16384]{0:T(1024)S(1)}, f32[16384]{0:T(1024)S(1)}, f32[]{:T(128)}, f32[16384]{0:T(1024)S(1)}, /*index=5*/f32[]{:T(128)}, f32[16384]{0:T(1024)S(1)}, f32[]{:T(128)}) fusion(bf16[1,4,16,16384]{3,2,1,0:T(8,128)(2,1)} %param.3), kind=kLoop, calls=%fused_computation.8 | loop fusion | flops 4128764 | bytes 2359312 | tf_op jit(solution)/shard_map/reduce_sum | solution.py:36
  9.9 0.5 collective-permute-start
  10.3 0.0 collective-permute-start.1
  10.4 0.5 collective-permute-start.2
  10.9 0.0 collective-permute-start.3
  10.9 35.8 %all-reduce = (f32[]{:T(128)}, f32[]{:T(128)}, f32[]{:T(128)}, f32[]{:T(128)}) all-reduce(f32[]{:T(128)} %get-tuple-element.12, f32[]{:T(128)} %get-tuple-element.10, f32[]{:T(128)} %get-tuple-element.8, f32[]{:T(128)} %get-tuple-element.5), channel_id=1, replica_groups=mesh['shard'=16,'task'=2] {'shard'}, use_global_device_ids=true, to_apply=%region_18.19 | all-reduce | flops 4 | bytes 32 | tf_op jit(solution)/shard_map/psum | solution.py:36
  49.2 0.0 copy-done.1
  49.2 0.7 fusion.27
  49.9 0.0 collective-permute-done
  50.0 0.0 collective-permute-done.1
  50.0 0.0 collective-permute-done.2
  50.1 0.0 collective-permute-done.3
  50.1 0.0 copy-done
  50.2 7.1 %fusion.9 = (f32[1,16,16384]{2,1,0:T(8,128)}, f32[1,16,16384]{2,1,0:T(8,128)}, f32[1,16,16384]{2,1,0:T(8,128)}, f32[1,16,16384]{2,1,0:T(8,128)}) fusion(s32[1,4,16,16384]{3,2,1,0:T(8,128)} %param.4, f32[16384]{0:T(1024)S(1)} %convert_element_type.104, s32[]{:T(128)} %get-tuple-element.13, bf16[1,4,16,16384]{3,2,1,0:T(8,128)(2,1)S(1)} %copy-done, ...), kind=kLoop, calls=%fused_computation.17 | loop fusion | flops 4194304 | bytes 10747920 | tf_op jit(solution)/shard_map/jit(_where)/select_n | solution.py:40
  57.3 0.0 all-gather.5.cloned.1.call-update
  57.3 0.0 all-gather.7.cloned.1.call-start
  57.4 0.7 all-gather.7.cloned.1.call-update
  58.1 0.0 all-gather.11.cloned.1.call-start
  58.1 0.7 all-gather.11.cloned.1.call-update
  58.8 0.0 all-gather.9.cloned.1.call-start
  58.9 0.5 all-gather.9.cloned.1.call-update
  59.4 28.5 %all-gather.5.cloned.1.call-done = f32[2,16,16384]{2,1,0:T(8,128)} async-done(((f32[1,16,16384]{2,1,0:T(8,128)}), f32[2,16,16384]{2,1,0:T(8,128)}) %all-gather.5.cloned.1.call-update) | async-done | bytes 2097168 | tf_op jit(solution)/shard_map/all_gather | solution.py:43
  87.8 1.7 reduce_sum.147
  89.6 32.9 %all-gather.7.cloned.1.call-done = f32[2,16,16384]{2,1,0:T(8,128)} async-done(((f32[1,16,16384]{2,1,0:T(8,128)}), f32[2,16,16384]{2,1,0:T(8,128)}) %all-gather.7.cloned.1.call-update) | async-done | bytes 2097168 | tf_op jit(solution)/shard_map/all_gather | solution.py:43
  122.5 1.7 reduce_sum.151
  124.3 32.9 %all-gather.11.cloned.1.call-done = f32[2,16,16384]{2,1,0:T(8,128)} async-done(((f32[1,16,16384]{2,1,0:T(8,128)}), f32[2,16,16384]{2,1,0:T(8,128)}) %all-gather.11.cloned.1.call-update) | async-done | bytes 2097168 | tf_op jit(solution)/shard_map/all_gather | solution.py:43
  157.2 1.7 reduce_sum.159
  159.0 32.7 %all-gather.9.cloned.1.call-done = f32[2,16,16384]{2,1,0:T(8,128)} async-done(((f32[1,16,16384]{2,1,0:T(8,128)}), f32[2,16,16384]{2,1,0:T(8,128)}) %all-gather.9.cloned.1.call-update) | async-done | bytes 2097168 | tf_op jit(solution)/shard_map/all_gather | solution.py:43
  191.7 1.7 reduce_sum.155
  193.5 1.1 pad_maximum_fusion
  (12 shorter events, 0.2 us)
Async XLA Ops:
  6.5 43.6 %copy-start = (bf16[1,4,16,16384]{3,2,1,0:T(8,128)(2,1)S(1)}, bf16[1,4,16,16384]{3,2,1,0:T(8,128)(2,1)}, u32[]{:S(2)}) copy-start(bf16[1,4,16,16384]{3,2,1,0:T(8,128)(2,1)} %param.3) | copy-start | bytes 6291460
  6.5 42.6 %copy-start.1 = (s32[1,4,8]{2,1,0:T(4,128)S(1)}, s32[1,4,8]{2,1,0:T(4,128)}, u32[]{:S(2)}) copy-start(s32[1,4,8]{2,1,0:T(4,128)} %param.5) | copy-start | bytes 388
  6.5 81.3 %all-gather.5.cloned.1.call-start = ((), (), s32[]{:S(2)}) async-start(), calls=%async_computation | async-start | bytes 3145728 | tf_op jit(solution)/shard_map/all_gather | solution.py:43
  9.9 40.1 %collective-permute-start = (f32[16384]{0:T(1024)S(1)}, f32[16384]{0:T(1024)S(1)}, u32[]{:S(2)}, u32[]{:S(2)}) collective-permute-start(f32[16384]{0:T(1024)S(1)} %get-tuple-element.6), channel_id=1, source_target_pairs={{0,2},{2,0},{4,6},{6,4},{8,10},{10,8},{12,14},{14,12},{16,18},{18,... | collective-permute-start | bytes 196616 | tf_op jit(solution)/shard_map/ppermute | solution.py:13
  10.3 39.6 %collective-permute-start.1 = (f32[16384]{0:T(1024)S(1)}, f32[16384]{0:T(1024)S(1)}, u32[]{:S(2)}, u32[]{:S(2)}) collective-permute-start(f32[16384]{0:T(1024)S(1)} %get-tuple-element.7), channel_id=1, source_target_pairs={{0,2},{2,0},{4,6},{6,4},{8,10},{10,8},{12,14},{14,12},{16,18},{18,... | collective-permute-start | bytes 196616 | tf_op jit(solution)/shard_map/ppermute | solution.py:13
  10.4 39.6 %collective-permute-start.2 = (f32[16384]{0:T(1024)S(1)}, f32[16384]{0:T(1024)S(1)}, u32[]{:S(2)}, u32[]{:S(2)}) collective-permute-start(f32[16384]{0:T(1024)S(1)} %get-tuple-element.9), channel_id=1, source_target_pairs={{0,2},{2,0},{4,6},{6,4},{8,10},{10,8},{12,14},{14,12},{16,18},{18,... | collective-permute-start | bytes 196616 | tf_op jit(solution)/shard_map/ppermute | solution.py:13
  10.9 39.2 %collective-permute-start.3 = (f32[16384]{0:T(1024)S(1)}, f32[16384]{0:T(1024)S(1)}, u32[]{:S(2)}, u32[]{:S(2)}) collective-permute-start(f32[16384]{0:T(1024)S(1)} %get-tuple-element.11), channel_id=1, source_target_pairs={{0,2},{2,0},{4,6},{6,4},{8,10},{10,8},{12,14},{14,12},{16,18},{18,... | collective-permute-start | bytes 196616 | tf_op jit(solution)/shard_map/ppermute | solution.py:13
  57.3 65.2 %all-gather.7.cloned.1.call-start = ((), (), s32[]{:S(2)}) async-start(), calls=%async_computation.1 | async-start | bytes 3145728 | tf_op jit(solution)/shard_map/all_gather | solution.py:43
  58.1 99.1 %all-gather.11.cloned.1.call-start = ((), (), s32[]{:S(2)}) async-start(), calls=%async_computation.3 | async-start | bytes 3145728 | tf_op jit(solution)/shard_map/all_gather | solution.py:43
  58.8 132.9 %all-gather.9.cloned.1.call-start = ((), (), s32[]{:S(2)}) async-start(), calls=%async_computation.2 | async-start | bytes 3145728 | tf_op jit(solution)/shard_map/all_gather | solution.py:43
Sparse Core Ops, SparseCore 0:
  57.4 30.3 all-gather.4
  89.4 33.0 all-gather.6
  124.1 33.0 all-gather.10
  158.6 33.0 all-gather.8
